TPU v7x, 32 devices: a whole 2x2x4 slice. The times are simulated.
32 devices in a mesh: cuts: 4 (over z), row: 8 (over y, x, core).
Axes of the slice: x: 2, y: 2, z: 4, core: 2. Of those that a mesh axis runs over, the one named last changes fastest.
Arguments:
- eigvecs: float32 [16384, 2048], P('row', 'cuts'), may hold values from -1.2 to 1.2
- slice_counts: int32 [4], P('cuts'), may hold values from 256 to 512, as said below
- occ_index: int32 [2048], P('cuts'), may hold values from 0 to 63
- occ_levels: float32 [64], replicated, may hold values from 0 to 1
Outputs:
- slab: float32 [4096, 16384], P('cuts', 'row')
Inputs may be any that keep to these rules, and one draw needn't show every extreme that they name: `slice_counts`: some slice holds exactly 512 eigenvalues in every draw; the others at least half of that.
All inputs are finite; a program needn't handle non-finite values.
Results may differ from a plain program's by a relative error of at most 0.000062.
Values sent between devices are 32-bit elements; how exact they have to be, the bound alone decides.
No kernel may reach another device: no remote copies, remote signals or barrier semaphores. Data moves between devices by JAX's collectives and lax.ppermute only.
A program may use at most 128 MiB of HBM per device.

v0:
```python
import jax
import jax.numpy as jnp
from jax import lax
from jax.sharding import PartitionSpec as P

BLOCK = 1024
SLAB_SUB = 256
SLAB = 4096


def shards(eigvecs, slice_counts, occ_index, occ_levels):
    row_count = eigvecs.shape[0]
    slot_count = eigvecs.shape[1]
    level_ids = jnp.arange(occ_levels.shape[0], dtype=jnp.int32)
    one_hot = (occ_index[:, None] == level_ids[None, :]).astype(jnp.float32)
    values = jnp.dot(one_hot, occ_levels, precision=lax.Precision.HIGHEST)
    live = jnp.arange(slot_count, dtype=jnp.int32) < slice_counts[0]
    weights = jnp.where(live, values, jnp.float32(0.0))
    local_blocks = eigvecs.reshape(row_count // BLOCK, BLOCK, slot_count)[:, :SLAB_SUB, :]
    local_rows = local_blocks.reshape(-1, slot_count) * weights[None, :]
    cut_count = lax.axis_size("cuts")
    row_devices = lax.axis_size("row")
    owned = SLAB // cut_count
    strip = slot_count // row_devices
    spread = lax.all_to_all(local_rows.T, "row", split_axis=0, concat_axis=1, tiled=True)
    owners = lax.all_to_all(spread, "cuts", split_axis=1, concat_axis=0, tiled=True)
    panels = lax.all_gather(owners, "row", axis=0, tiled=True)
    panel = (
        panels.reshape(row_devices, cut_count, strip, owned)
        .transpose(1, 0, 2, 3)
        .reshape(cut_count * slot_count, owned)
    )
    return lax.dot_general(
        panel,
        lax.all_gather(eigvecs, "cuts", axis=1, tiled=True),
        (((0,), (1,)), ((), ())),
        precision=lax.Precision.HIGHEST,
        preferred_element_type=jnp.float32,
    )


def solution(mesh):
    return jax.shard_map(
        shards,
        mesh=mesh,
        in_specs=(P("row", "cuts"), P("cuts"), P("cuts"), P()),
        out_specs=P("cuts", "row"),
        check_vma=False,
    )
```

profile of v0, /device:TPU:0, one launch (start us, length us, event | category | flops | bytes accessed | tf_op | source)
XLA Modules:
  0.0 519.5 jit_solution(15764011367793498607)
XLA Ops:
  6.5 0.0 copy-start
  6.5 0.0 all-gather.3.cloned.1.call-start
  7.2 1.3 slice.4
  8.5 0.3 copy.14
  8.8 0.0 copy-done
  8.9 1.0 fusion
  9.9 0.2 broadcast_multiply_fusion
  10.0 20.3 %all_to_all.35 = f32[8,64,512]{2,1,0:T(8,128)S(1)} all-to-all(f32[8,64,512]{2,1,0:T(8,128)S(1)} %bitcast.24), channel_id=1, replica_groups=mesh['cuts'=4,'row'=8] {'row'}, dimensions={0} | all-to-all | bytes 2097152 | tf_op jit(solution)/shard_map/all_to_all | solution.py:25
  30.3 0.6 copy.10
  31.0 0.5 all_to_all.29
  31.5 0.6 copy.11
  32.1 29.9 %all_to_all.36 = f32[64,4,1024]{2,0,1:T(8,128)} all-to-all(f32[64,4,1024]{2,0,1:T(8,128)S(1)} %copy.11), channel_id=1, replica_groups=mesh['cuts'=4,'row'=8] {'cuts'}, dimensions={1} | all-to-all | bytes 2097152 | tf_op jit(solution)/shard_map/all_to_all | solution.py:26
  62.0 0.0 all-gather.3.cloned.1.call-update
  62.1 0.0 all-gather.5.cloned.1.call-start
  62.1 0.7 all-gather.5.cloned.1.call-update
  62.8 51.5 %all-gather.3.cloned.1.call-done = f32[2048,1024]{1,0:T(8,128)} async-done(((f32[256,1024]{1,0:T(8,128)}), f32[2048,1024]{1,0:T(8,128)}) %all-gather.3.cloned.1.call-update) | async-done | bytes 8388624 | tf_op jit(solution)/shard_map/all_gather | solution.py:27
  114.3 8.3 %copy.12 = f32[8,4,64,1024]{3,2,0,1:T(8,128)} copy(f32[8,4,64,1024]{3,2,1,0:T(8,128)} %bitcast.21) | data formatting | bytes 16777216 | tf_op jit(solution)/shard_map/reshape | solution.py:29
  122.6 280.1 %all-gather.5.cloned.1.call-done = f32[2048,2048]{1,0:T(8,128)} async-done(((f32[2048,512]{1,0:T(8,128)}), f32[2048,2048]{1,0:T(8,128)}) %all-gather.5.cloned.1.call-update) | async-done | bytes 16777232 | tf_op jit(solution)/shard_map/all_gather | solution.py:35
  402.7 110.0 %fusion.4 = f32[1024,2048]{1,0:T(8,128)} fusion(f32[2048,1024]{1,0:T(8,128)} %bitcast.22, f32[2048,2048]{1,0:T(8,128)} %all-gather.5.cloned.1.call-done), kind=kOutput, calls=%fused_computation.7 | convolution fusion | flops 51539607552 | bytes 33554432 | tf_op jit(solution)/shard_map/dot_general | solution.py:33
  (1 shorter events, 0.0 us)
Async XLA Ops:
  6.5 2.3 copy-start
  6.5 107.8 %all-gather.3.cloned.1.call-start = ((), (), s32[]{:S(2)}) async-start(), calls=%async_computation.2 | async-start | bytes 9437184 | tf_op jit(solution)/shard_map/all_gather | solution.py:27
  62.1 340.6 %all-gather.5.cloned.1.call-start = ((), (), s32[]{:S(2)}) async-start(), calls=%async_computation.3 | async-start | bytes 20971520 | tf_op jit(solution)/shard_map/all_gather | solution.py:35
Sparse Core Ops, SparseCore 0:
  62.2 52.0 all-gather.2
  115.9 286.7 all-gather.4
where the time goes:
time: 520 us; the launch traced here: 519 us
  waiting for transfers between devices  332 us (64%)
  matrix products  111 us (21%)
  blocking collectives  50.3 us (10%)
  between operations  14.1 us (3%)
  local copies, waits for them, and re-layouts  11.6 us (2%)
    all_gather x1, waiting for transfers between devices, shards(): lax.all_gather(eigvecs, 'cuts', axis=1, tiled=True)  280 us
    dot_general x1, matrix products, shards(): lax.dot_general(panel, lax.all_gather(eigvecs, 'cuts', axis=1, tiled=True...  110 us
    all_gather x1, waiting for transfers between devices, shards(): panels = lax.all_gather(owners, 'row', axis=0, tiled=True)  51.5 us
    all_to_all x1, blocking collectives, shards(): lax.all_to_all(spread, 'cuts', split_axis=1, concat_axis=0, tiled=True)  29.9 us
    all_to_all x1, blocking collectives, shards(): lax.all_to_all(local_rows.T, 'row', split_axis=0, concat_axis=1, tiled=True)  20.3 us
  transfers between devices with their start and end apart: 2, of which 2 were waited for; matrix products, arithmetic and copies ran while one was open for 2% of the time, Pallas kernels for 0%

commit v1 on v0

--- a/solution.py
+++ b/solution.py
@@ -6,6 +6,11 @@
 BLOCK = 1024
 SLAB_SUB = 256
 SLAB = 4096
+
+
+def gathered_along(x, axis, dim):
+    blocks = lax.all_gather(x, axis)
+    return jnp.concatenate(blocks, axis=dim)
 
 
 def shards(eigvecs, slice_counts, occ_index, occ_levels):
@@ -32,7 +37,7 @@
     )
     return lax.dot_general(
         panel,
-        lax.all_gather(eigvecs, "cuts", axis=1, tiled=True),
+        gathered_along(eigvecs, "cuts", 1),
         (((0,), (1,)), ((), ())),
         precision=lax.Precision.HIGHEST,
         preferred_element_type=jnp.float32,

time: 520 us -> 485 us (0.933)
  matrix products: 111 us -> 59.7 us
  local copies, waits for them, and re-layouts: 11.6 us -> 28 us
    dot_general x1, matrix products: 110 us -> 58.7 us  [shards(): lax.dot_general(panel, gathered_along(eigvecs, 'cuts', 1), (((0,), (1,)),...]
    reshape x0 -> x1, local copies, waits for them, and re-layouts: none -> 16.3 us  [gathered_along(): return jnp.concatenate(blocks, axis=dim)]
where the time goes in v1:
time: 485 us
  waiting for transfers between devices  332 us (68%)
  matrix products  59.7 us (12%)
  blocking collectives  50.3 us (10%)
  local copies, waits for them, and re-layouts  28 us (6%)
  between operations  14.1 us (3%)
    all_gather x1, waiting for transfers between devices, gathered_along(): blocks = lax.all_gather(x, axis)  280 us
    dot_general x1, matrix products, shards(): lax.dot_general(panel, gathered_along(eigvecs, 'cuts', 1), (((0,), (1,)),...  58.7 us
    all_gather x1, waiting for transfers between devices, shards(): panels = lax.all_gather(owners, 'row', axis=0, tiled=True)  51.5 us
    all_to_all x1, blocking collectives, shards(): lax.all_to_all(spread, 'cuts', split_axis=1, concat_axis=0, tiled=True)  29.9 us
    all_to_all x1, blocking collectives, shards(): lax.all_to_all(local_rows.T, 'row', split_axis=0, concat_axis=1, tiled=True)  20.3 us
    reshape x1, local copies, waits for them, and re-layouts, gathered_along(): return jnp.concatenate(blocks, axis=dim)  16.3 us
  transfers between devices with their start and end apart: 2, of which 2 were waited for; matrix products, arithmetic and copies ran while one was open for 2% of the time, Pallas kernels for 0%

profile of v1, /device:TPU:0, one launch (start us, length us, event | category | flops | bytes accessed | tf_op | source)
XLA Modules:
  0.0 484.6 jit_solution(17889771841809579539)
XLA Ops:
  6.5 0.0 copy-start
  6.5 0.0 all-gather.4.cloned.1.call-start
  6.5 1.3 slice.4
  7.8 0.3 copy.20
  8.8 0.0 copy-done
  8.8 1.0 fusion
  9.8 0.2 broadcast_multiply_fusion
  10.0 20.3 %all_to_all.35 = f32[8,64,512]{2,1,0:T(8,128)S(1)} all-to-all(f32[8,64,512]{2,1,0:T(8,128)S(1)} %bitcast.30), channel_id=1, replica_groups=mesh['cuts'=4,'row'=8] {'row'}, dimensions={0} | all-to-all | bytes 2097152 | tf_op jit(solution)/shard_map/all_to_all | solution.py:30
  30.3 0.6 copy.15
  30.9 0.5 all_to_all.29
  31.5 0.6 copy.16
  32.1 29.9 %all_to_all.36 = f32[64,4,1024]{2,0,1:T(8,128)} all-to-all(f32[64,4,1024]{2,0,1:T(8,128)S(1)} %copy.16), channel_id=1, replica_groups=mesh['cuts'=4,'row'=8] {'cuts'}, dimensions={1} | all-to-all | bytes 2097152 | tf_op jit(solution)/shard_map/all_to_all | solution.py:31
  62.0 0.0 all-gather.4.cloned.1.call-update
  62.1 0.0 all-gather.6.cloned.1.call-start
  62.1 0.7 all-gather.6.cloned.1.call-update
  62.8 51.5 %all-gather.4.cloned.1.call-done = f32[2048,1024]{1,0:T(8,128)} async-done(((f32[256,1024]{1,0:T(8,128)}), f32[2048,1024]{1,0:T(8,128)}) %all-gather.4.cloned.1.call-update) | async-done | bytes 8388624 | tf_op jit(solution)/shard_map/all_gather | solution.py:32
  114.3 8.3 %copy.17 = f32[8,4,64,1024]{3,2,0,1:T(8,128)} copy(f32[8,4,64,1024]{3,2,1,0:T(8,128)} %bitcast.27) | data formatting | bytes 16777216 | tf_op jit(solution)/shard_map/reshape | solution.py:34
  122.6 280.1 %all-gather.6.cloned.1.call-done = f32[8192,512]{1,0:T(8,128)} async-done(((f32[2048,512]{1,0:T(8,128)}), f32[8192,512]{1,0:T(8,128)}) %all-gather.6.cloned.1.call-update) | async-done | bytes 16777232 | tf_op jit(solution)/shard_map/all_gather | solution.py:12
  402.7 16.3 %copy.18 = f32[2048,4,512]{0,2,1:T(8,128)} copy(f32[2048,4,512]{2,0,1:T(8,128)} %bitcast.25) | data formatting | bytes 33554432 | tf_op jit(solution)/shard_map/reshape | solution.py:13
  419.0 0.0 copy-start.1
  419.0 58.7 %fusion.4 = f32[1024,2048]{1,0:T(8,128)} fusion(f32[2048,1024]{1,0:T(8,128)} %bitcast.28, f32[2048,2048]{0,1:T(8,128)} %bitcast.26), kind=kOutput, calls=%fused_computation.7 | convolution fusion | flops 51539607552 | bytes 33554432 | tf_op jit(solution)/shard_map/dot_general | solution.py:38
  477.7 0.0 copy-done.1
  (1 shorter events, 0.0 us)
Async XLA Ops:
  6.5 2.3 copy-start
  6.5 107.8 %all-gather.4.cloned.1.call-start = ((), (), s32[]{:S(2)}) async-start(), calls=%async_computation.2 | async-start | bytes 9437184 | tf_op jit(solution)/shard_map/all_gather | solution.py:32
  62.1 340.6 %all-gather.6.cloned.1.call-start = ((), (), s32[]{:S(2)}) async-start(), calls=%async_computation.3 | async-start | bytes 20971520 | tf_op jit(solution)/shard_map/all_gather | solution.py:12
  419.0 58.7 %copy-start.1 = (f32[64]{0:T(128)S(1)}, f32[64]{0:T(128)}, u32[]{:S(2)}) copy-start(f32[64]{0:T(128)} %param.7) | copy-start | bytes 772
Sparse Core Ops, SparseCore 0:
  62.2 52.0 all-gather.3
  115.9 286.7 all-gather.5
